TPU v7x, 32 devices: a whole 2x2x4 slice. The times are simulated.
32 devices in a mesh: seq: 8 (over y, x, core), fsdp: 4 (over z).
Axes of the slice: x: 2, y: 2, z: 4, core: 2. Of those that a mesh axis runs over, the one named last changes fastest.
Arguments:
- hidden: bfloat16 [4096, 8192], P(('seq', 'fsdp')), may hold values from -6 to 6
- kv_blocks: bfloat16 [8192, 1024], P('fsdp'), may hold values from -0.0625 to 0.0625
- kv_scale: float32 [64, 8], P('fsdp'), may hold values from 0.5 to 2
- queries: bfloat16 [4096, 4096], P(('seq', 'fsdp')), may hold values from -24 to 24
- grad_out: bfloat16 [4096, 4096], P(('seq', 'fsdp')), may hold values from -6 to 6
Outputs:
- attn_out: bfloat16 [4096, 4096], P(('seq', 'fsdp'))
- grad_queries: bfloat16 [4096, 4096], P(('seq', 'fsdp'))
- grad_hidden: bfloat16 [4096, 8192], P(('seq', 'fsdp'))
- weight_grad: float32 [8192, 1024], P('fsdp')
All inputs are finite; a program needn't handle non-finite values.
Results may differ from a plain program's by a relative error of at most 0.0075.
The roundings to bfloat16 on the way count: a program that leaves them out, or rounds other values in their place, can miss the bound.
Values may be sent and summed in bfloat16 or wider, within the bound.
A program may use at most 128 MiB of HBM per device.

v0:
```python
import jax
import jax.numpy as jnp
from jax import lax
from jax.sharding import PartitionSpec as P

HEADS = 32
KV_HEADS = 4
HEAD = 128
QB = 128
NEG = -1e30


def shifted(block, axis, distance):
    devices = range(lax.axis_size(axis))
    route = [(i - distance, i) for i in devices if i - distance in devices]
    return lax.ppermute(block, axis, route)


def dequantize(blocks, scale):
    rows, cols = blocks.shape
    grid = blocks.astype(jnp.float32).reshape(scale.shape[0], QB, scale.shape[1], QB)
    return (grid * scale[:, None, :, None]).reshape(rows, cols).astype(jnp.bfloat16)


def attend_group(operands, allowed):
    qgrp, kgrp, vgrp, ggrp = operands
    factor = 1.0 / float(HEAD) ** 0.5
    scores = jnp.einsum("rhd,kd->rhk", qgrp, kgrp, preferred_element_type=jnp.float32) * factor
    scores = jnp.where(allowed[:, None, :], scores, NEG)
    top = jnp.max(scores, axis=-1, keepdims=True)
    expd = jnp.exp(scores - top)
    probs = expd / jnp.sum(expd, axis=-1, keepdims=True)
    probs_b = probs.astype(jnp.bfloat16)
    output = jnp.einsum("rhk,kd->rhd", probs_b, vgrp, preferred_element_type=jnp.float32).astype(
        jnp.bfloat16
    )
    dprobs = jnp.einsum("rhd,kd->rhk", ggrp, vgrp, preferred_element_type=jnp.float32)
    delta = jnp.sum(probs * dprobs, axis=-1, keepdims=True)
    dscores = (probs * (dprobs - delta) * factor).astype(jnp.bfloat16)
    gradq = jnp.einsum("rhk,kd->rhd", dscores, kgrp, preferred_element_type=jnp.float32).astype(
        jnp.bfloat16
    )
    gradk = jnp.einsum("rhk,rhd->kd", dscores, qgrp, preferred_element_type=jnp.float32)
    gradv = jnp.einsum("rhk,rhd->kd", probs_b, ggrp, preferred_element_type=jnp.float32)
    return (output, gradq, gradk, gradv)


def attend(queries, window, grad_out, allowed):
    rows = queries.shape[0]
    count = window.shape[0]
    group = HEADS // KV_HEADS
    kvw = KV_HEADS * HEAD
    qgrp = queries.reshape(rows, KV_HEADS, group, HEAD).transpose(1, 0, 2, 3)
    ggrp = grad_out.reshape(rows, KV_HEADS, group, HEAD).transpose(1, 0, 2, 3)
    kgrp = window[:, :kvw].reshape(count, KV_HEADS, HEAD).transpose(1, 0, 2)
    vgrp = window[:, kvw:].reshape(count, KV_HEADS, HEAD).transpose(1, 0, 2)
    output, gradq, gradk, gradv = lax.map(
        lambda ops: attend_group(ops, allowed), (qgrp, kgrp, vgrp, ggrp)
    )
    output = output.transpose(1, 0, 2, 3).reshape(rows, HEADS * HEAD)
    gradq = gradq.transpose(1, 0, 2, 3).reshape(rows, HEADS * HEAD)
    gradk = gradk.transpose(1, 0, 2).reshape(count, kvw)
    gradv = gradv.transpose(1, 0, 2).reshape(count, kvw)
    return (output, gradq, jnp.concatenate([gradk, gradv], axis=1))


def body(hidden, kv_blocks, kv_scale, queries, grad_out):
    tok = hidden.shape[0]
    groups = lax.axis_size("fsdp")
    reach = groups // 2
    place = lax.axis_index("fsdp")
    linear = lax.axis_index("seq") * groups + place
    weights = dequantize(kv_blocks, kv_scale)
    columns = lax.all_to_all(hidden, "fsdp", split_axis=1, concat_axis=0, tiled=True)
    rows = columns
    kv = lax.psum_scatter(
        jnp.dot(rows, weights, preferred_element_type=jnp.float32),
        "fsdp",
        scatter_dimension=0,
        tiled=True,
    ).astype(jnp.bfloat16)
    pieces = []
    for offset in range(reach, 0, -1):
        pieces.append(shifted(kv, ("seq", "fsdp"), offset))
    window = jnp.concatenate(pieces + [kv], axis=0)
    base = linear * tok
    qpos = base + jnp.arange(tok, dtype=jnp.int32)
    kpos = base - reach * tok + jnp.arange((reach + 1) * tok, dtype=jnp.int32)
    span = reach * tok
    allowed = (
        (qpos[:, None] - kpos[None, :] < span)
        & (kpos[None, :] <= qpos[:, None])
        & (kpos[None, :] >= 0)
    )
    attn_out, grad_queries, dwin = attend(queries, window, grad_out, allowed)
    total = dwin[reach * tok :]
    inside = total
    for offset in range(1, reach + 1):
        piece = dwin[(reach - offset) * tok : (reach - offset + 1) * tok]
        returned = shifted(piece, ("seq", "fsdp"), -offset)
        total = total + returned
        inside = inside + jnp.where(place + offset < groups, returned, jnp.zeros_like(returned))
    all_grad = total.astype(jnp.bfloat16)
    seg_grad = inside.astype(jnp.bfloat16)
    spread = lax.dot_general(
        lax.all_gather(seg_grad, "fsdp", axis=0, tiled=True),
        weights,
        (((1,), (1,)), ((), ())),
        preferred_element_type=jnp.float32,
    ).astype(jnp.bfloat16)
    grad_hidden = lax.all_to_all(spread, "fsdp", split_axis=0, concat_axis=1, tiled=True)
    rows = columns
    shard_grad = lax.dot_general(
        rows,
        lax.all_gather(all_grad, "fsdp", axis=0, tiled=True),
        (((0,), (0,)), ((), ())),
        preferred_element_type=jnp.float32,
    )
    weight_grad = lax.psum(shard_grad, "seq")
    return (attn_out, grad_queries, grad_hidden, weight_grad)


def solution(mesh):
    return jax.shard_map(
        body,
        mesh=mesh,
        in_specs=(
            P(("seq", "fsdp"), None),
            P("fsdp", None),
            P("fsdp", None),
            P(("seq", "fsdp"), None),
            P(("seq", "fsdp"), None),
        ),
        out_specs=(
            P(("seq", "fsdp"), None),
            P(("seq", "fsdp"), None),
            P(("seq", "fsdp"), None),
            P("fsdp", None),
        ),
        check_vma=False,
    )
```

profile of v0, /device:TPU:0, one launch (start us, length us, event | category | flops | bytes accessed | tf_op | source)
XLA Modules:
  0.0 503.2 jit_solution(12745964746301407682)
XLA Ops:
  7.2 4.1 copy.37
  11.2 6.5 %all-to-all-start = ((bf16[128,4,2048]{0,2,1:T(8,128)(2,1)}), bf16[128,4,2048]{0,2,1:T(8,128)(2,1)S(1)}, u32[]{:S(2)}, u32[]{:S(2)}) async-start(bf16[128,4,2048]{0,2,1:T(8,128)(2,1)} %bitcast.160), calls=%async_computation | async-start | bytes 4194304 | tf_op jit(solution)/shard_map/all_to_all | solution.py:74
  17.8 48.1 %all-to-all-done = bf16[128,4,2048]{0,2,1:T(8,128)(2,1)S(1)} async-done(((bf16[128,4,2048]{0,2,1:T(8,128)(2,1)}), bf16[128,4,2048]{0,2,1:T(8,128)(2,1)S(1)}, u32[]{:S(2)}, u32[]{:S(2)}) %all-to-all-start) | async-done | bytes 2097184 | tf_op jit(solution)/shard_map/all_to_all | solution.py:74
  69.1 4.2 copy-done
  74.4 4.0 convolution_bitcast_fusion.2
  78.5 42.8 %reduce-scatter.2.cloned.1.call-done = f32[128,1024]{0,1:T(8,128)} async-done(((f32[512,1024]{0,1:T(8,128)}), f32[128,1024]{0,1:T(8,128)}) %reduce-scatter.2.cloned.1.call-update) | async-done | bytes 524304 | tf_op jit(solution)/shard_map/reduce_scatter | solution.py:76
  125.0 4.3 collective-permute-start
  137.0 110.8 %while.17 = (s32[]{:T(128)}, bf16[4,128,8,128]{3,1,2,0:T(8,128)(2,1)}, bf16[4,128,8,128]{3,1,2,0:T(8,128)(2,1)}, f32[4,384,128]{1,2,0:T(8,128)S(1)}, f32[4,384,1...) while((s32[]{:T(128)}, ...), condition=%wide.region_5.6_spmd.clone, body=%wide.region_1.5_spmd.clone.sunk | while | flops 816830336 | bytes 25336436 | solution.py:57
  140.2 3.8 fusion.153
  145.2 8.0 %fusion.155 = bf16[4,128,8,128]{3,1,2,0:T(8,128)(2,1)} fusion(bf16[4,128,8,128]{3,1,2,0:T(8,128)(2,1)} %get-tuple-element.254, s32[]{:T(128)S(6)} %copy.76, f32[128,8,384]{2,0,1:T(8,128)S(1)} %fusion.154, bf16[4,384,128]{2,1,0:T(8,128)(2,1)} %copy-done.9, f32[128,8,384]{2,0,1:T(8,128)} %get-tuple-element.238, f32[128,8]{0,1:T(8,128)S(1)} %get-tuple-element.237), kind=kOutput, calls=%fused_computation.16.clone.1 | convolution fusion | flops 103548288 | bytes 6661120 | tf_op jit(solution)/shard_map/while/body/eval_jaxpr/rhk,kd->rhd/dot_general | solution.py:40
  153.2 7.5 %fusion.156 = f32[4,384,128]{1,2,0:T(8,128)S(1)} fusion(f32[4,384,128]{1,2,0:T(8,128)S(1)} %get-tuple-element.255, s32[]{:T(128)S(6)} %copy.76, f32[128,8,384]{2,0,1:T(8,128)S(1)} %fusion.154, bf16[4,128,8,128]{1,3,2,0:T(8,128)(2,1)} %get-tuple-element.270, f32[128,8,384]{2,0,1:T(8,128)} %get-tuple-element.238, f32[128,8]{0,1:T(8,128)S(1)} %get-tuple-element.237), kind=kOutput, calls=%fused_computation.20.clone.1 | convolution fusion | flops 103417216 | bytes 6759424 | tf_op jit(solution)/shard_map/while/body/eval_jaxpr/rhk,rhd->kd/dot_general | solution.py:43
  160.7 4.0 fusion.157
  167.8 3.8 fusion.153
  172.9 8.0 %fusion.155 = bf16[4,128,8,128]{3,1,2,0:T(8,128)(2,1)} fusion(bf16[4,128,8,128]{3,1,2,0:T(8,128)(2,1)} %get-tuple-element.254, s32[]{:T(128)S(6)} %copy.76, f32[128,8,384]{2,0,1:T(8,128)S(1)} %fusion.154, bf16[4,384,128]{2,1,0:T(8,128)(2,1)} %copy-done.9, f32[128,8,384]{2,0,1:T(8,128)} %get-tuple-element.238, f32[128,8]{0,1:T(8,128)S(1)} %get-tuple-element.237), kind=kOutput, calls=%fused_computation.16.clone.1 | convolution fusion | flops 103548288 | bytes 6661120 | tf_op jit(solution)/shard_map/while/body/eval_jaxpr/rhk,kd->rhd/dot_general | solution.py:40
  180.9 7.5 %fusion.156 = f32[4,384,128]{1,2,0:T(8,128)S(1)} fusion(f32[4,384,128]{1,2,0:T(8,128)S(1)} %get-tuple-element.255, s32[]{:T(128)S(6)} %copy.76, f32[128,8,384]{2,0,1:T(8,128)S(1)} %fusion.154, bf16[4,128,8,128]{1,3,2,0:T(8,128)(2,1)} %get-tuple-element.270, f32[128,8,384]{2,0,1:T(8,128)} %get-tuple-element.238, f32[128,8]{0,1:T(8,128)S(1)} %get-tuple-element.237), kind=kOutput, calls=%fused_computation.20.clone.1 | convolution fusion | flops 103417216 | bytes 6759424 | tf_op jit(solution)/shard_map/while/body/eval_jaxpr/rhk,rhd->kd/dot_general | solution.py:43
  188.4 4.0 fusion.157
  195.5 3.8 fusion.153
  200.6 8.0 %fusion.155 = bf16[4,128,8,128]{3,1,2,0:T(8,128)(2,1)} fusion(bf16[4,128,8,128]{3,1,2,0:T(8,128)(2,1)} %get-tuple-element.254, s32[]{:T(128)S(6)} %copy.76, f32[128,8,384]{2,0,1:T(8,128)S(1)} %fusion.154, bf16[4,384,128]{2,1,0:T(8,128)(2,1)} %copy-done.9, f32[128,8,384]{2,0,1:T(8,128)} %get-tuple-element.238, f32[128,8]{0,1:T(8,128)S(1)} %get-tuple-element.237), kind=kOutput, calls=%fused_computation.16.clone.1 | convolution fusion | flops 103548288 | bytes 6661120 | tf_op jit(solution)/shard_map/while/body/eval_jaxpr/rhk,kd->rhd/dot_general | solution.py:40
  208.5 7.5 %fusion.156 = f32[4,384,128]{1,2,0:T(8,128)S(1)} fusion(f32[4,384,128]{1,2,0:T(8,128)S(1)} %get-tuple-element.255, s32[]{:T(128)S(6)} %copy.76, f32[128,8,384]{2,0,1:T(8,128)S(1)} %fusion.154, bf16[4,128,8,128]{1,3,2,0:T(8,128)(2,1)} %get-tuple-element.270, f32[128,8,384]{2,0,1:T(8,128)} %get-tuple-element.238, f32[128,8]{0,1:T(8,128)S(1)} %get-tuple-element.237), kind=kOutput, calls=%fused_computation.20.clone.1 | convolution fusion | flops 103417216 | bytes 6759424 | tf_op jit(solution)/shard_map/while/body/eval_jaxpr/rhk,rhd->kd/dot_general | solution.py:43
  216.1 4.0 fusion.157
  228.3 8.0 %fusion.155 = bf16[4,128,8,128]{3,1,2,0:T(8,128)(2,1)} fusion(bf16[4,128,8,128]{3,1,2,0:T(8,128)(2,1)} %get-tuple-element.254, s32[]{:T(128)S(6)} %copy.76, f32[128,8,384]{2,0,1:T(8,128)S(1)} %fusion.154, bf16[4,384,128]{2,1,0:T(8,128)(2,1)} %copy-done.9, f32[128,8,384]{2,0,1:T(8,128)} %get-tuple-element.238, f32[128,8]{0,1:T(8,128)S(1)} %get-tuple-element.237), kind=kOutput, calls=%fused_computation.16.clone.1 | convolution fusion | flops 103548288 | bytes 6661120 | tf_op jit(solution)/shard_map/while/body/eval_jaxpr/rhk,kd->rhd/dot_general | solution.py:40
  236.2 7.5 %fusion.156 = f32[4,384,128]{1,2,0:T(8,128)S(1)} fusion(f32[4,384,128]{1,2,0:T(8,128)S(1)} %get-tuple-element.255, s32[]{:T(128)S(6)} %copy.76, f32[128,8,384]{2,0,1:T(8,128)S(1)} %fusion.154, bf16[4,128,8,128]{1,3,2,0:T(8,128)(2,1)} %get-tuple-element.270, f32[128,8,384]{2,0,1:T(8,128)} %get-tuple-element.238, f32[128,8]{0,1:T(8,128)S(1)} %get-tuple-element.237), kind=kOutput, calls=%fused_computation.20.clone.1 | convolution fusion | flops 103417216 | bytes 6759424 | tf_op jit(solution)/shard_map/while/body/eval_jaxpr/rhk,rhd->kd/dot_general | solution.py:43
  243.8 4.0 fusion.157
  252.3 32.5 %collective-permute-done.3 = f32[128,1024]{0,1:T(8,128)} collective-permute-done((f32[128,1024]{0,1:T(8,128)}, f32[128,1024]{0,1:T(8,128)}, u32[]{:S(2)}, u32[]{:S(2)}) %collective-permute-start.3) | collective-permute-done | bytes 524320 | tf_op jit(solution)/shard_map/ppermute | solution.py:16
  288.2 41.5 %all-gather.5.cloned.1.call-done = bf16[512,1024]{0,1:T(8,128)(2,1)} async-done(((bf16[128,1024]{0,1:T(8,128)(2,1)}), bf16[512,1024]{0,1:T(8,128)(2,1)}) %all-gather.5.cloned.1.call-update) | async-done | bytes 1048592 | tf_op jit(solution)/shard_map/all_gather | solution.py:115
  329.7 6.8 %convolution_bitcast_fusion.1 = f32[2048,1024]{0,1:T(8,128)} fusion(bf16[512,1024]{0,1:T(8,128)(2,1)} %all-gather.5.cloned.1.call-done, bf16[512,2048]{1,0:T(8,128)(2,1)S(1)} %bitcast.162), kind=kOutput, calls=%fused_computation.64 | convolution fusion | flops 2147483648 | bytes 11534336 | tf_op jit(solution)/shard_map/dot_general | solution.py:113
  336.5 23.0 %all-gather.3.cloned.1.call-done = bf16[512,1024]{0,1:T(8,128)(2,1)} async-done(((bf16[128,1024]{0,1:T(8,128)(2,1)}), bf16[512,1024]{0,1:T(8,128)(2,1)}) %all-gather.3.cloned.1.call-update) | async-done | bytes 1048592 | tf_op jit(solution)/shard_map/all_gather | solution.py:106
  359.6 9.0 %convolution_convert_fusion.1 = bf16[512,2048]{1,0:T(8,128)(2,1)} fusion(bf16[512,1024]{0,1:T(8,128)(2,1)} %all-gather.3.cloned.1.call-done, f32[256,8,8,128]{3,2,1,0:T(8,128)} %bitcast.157, bf16[2048,1024]{1,0:T(8,128)(2,1)} %param.8), kind=kOutput, calls=%fused_computation.65 | convolution fusion | flops 2154823680 | bytes 15728640 | tf_op jit(solution)/shard_map/dot_general | solution.py:105
  368.6 3.9 all-to-all-start.1
  376.7 42.7 %all-to-all-done.1 = bf16[4,128,2048]{2,1,0:T(8,128)(2,1)S(1)} async-done(((bf16[4,128,2048]{2,1,0:T(8,128)(2,1)}), bf16[4,128,2048]{2,1,0:T(8,128)(2,1)S(1)}, u32[]{:S(2)}, u32[]{:S(2)}) %all-to-all-start.1) | async-done | bytes 2097184 | tf_op jit(solution)/shard_map/all_to_all | solution.py:111
  420.9 66.5 %all-reduce.2.cloned.1.call-done = f32[2048,1024]{0,1:T(8,128)} async-done(((f32[2048,1024]{0,1:T(8,128)}), f32[2048,1024]{0,1:T(8,128)}) %all-reduce.2.cloned.1.call-update) | async-done | bytes 8388624 | tf_op jit(solution)/shard_map/psum | solution.py:119
  487.4 9.2 %copy.49 = f32[2048,1024]{1,0:T(8,128)} copy(f32[2048,1024]{0,1:T(8,128)} %all-reduce.2.cloned.1.call-done) | data formatting | bytes 16777216
  (97 shorter events, 50.5 us)
Async XLA Ops:
  11.2 6.5 %copy-start.11 = (f32[16,8]{0,1:T(8,128)S(1)}, f32[16,8]{0,1:T(8,128)}, u32[]{:S(2)}) copy-start(f32[16,8]{0,1:T(8,128)} %param.9) | copy-start | bytes 1540
  11.2 54.7 %all-to-all-start = ((bf16[128,4,2048]{0,2,1:T(8,128)(2,1)}), bf16[128,4,2048]{0,2,1:T(8,128)(2,1)S(1)}, u32[]{:S(2)}, u32[]{:S(2)}) async-start(bf16[128,4,2048]{0,2,1:T(8,128)(2,1)} %bitcast.160), calls=%async_computation | async-start | bytes 4194304 | tf_op jit(solution)/shard_map/all_to_all | solution.py:74
  17.7 103.6 %reduce-scatter.2.cloned.1.call-start = ((), (), s32[]{:S(2)}) async-start(), calls=%async_computation.3 | async-start | bytes 2621440 | tf_op jit(solution)/shard_map/reduce_scatter | solution.py:76
  68.5 4.9 copy-start.1
  68.5 5.9 %copy-start.2 = (bf16[4,128,2048]{2,1,0:T(8,128)(2,1)S(1)}, bf16[4,128,2048]{2,1,0:T(8,128)(2,1)}, u32[]{:S(2)}) copy-start(bf16[4,128,2048]{2,1,0:T(8,128)(2,1)} %copy.38) | copy-start | bytes 6291460
  69.1 4.3 copy-start
  78.4 50.9 %copy-start.6 = (bf16[128,4096]{1,0:T(8,128)(2,1)S(1)}, bf16[128,4096]{1,0:T(8,128)(2,1)}, u32[]{:S(2)}) copy-start(bf16[128,4096]{1,0:T(8,128)(2,1)} %param.10) | copy-start | bytes 3145732
  78.4 251.3 %all-gather.5.cloned.1.call-start = ((), (), s32[]{:S(2)}) async-start(), calls=%async_computation.5 | async-start | bytes 1310720 | tf_op jit(solution)/shard_map/all_gather | solution.py:115
  122.4 9.8 %collective-permute-start.1 = (bf16[128,1024]{0,1:T(8,128)(2,1)S(1)}, bf16[128,1024]{0,1:T(8,128)(2,1)S(1)}, u32[]{:S(2)}, u32[]{:S(2)}) collective-permute-start(bf16[128,1024]{0,1:T(8,128)(2,1)S(1)} %convert_element_type.32), channel_id=1, source_target_pairs={{0,1},{1,2},{2,3},{3,4},{4,5},{5,6},{6,7},{7,8},{8,9},{9,10},{10,1... | collective-permute-start | bytes 786440 | tf_op jit(solution)/shard_map/ppermute | solution.py:16
  125.0 10.4 %collective-permute-start = (bf16[128,1024]{0,1:T(8,128)(2,1)S(1)}, bf16[128,1024]{0,1:T(8,128)(2,1)}, u32[]{:S(2)}, u32[]{:S(2)}) collective-permute-start(bf16[128,1024]{0,1:T(8,128)(2,1)S(1)} %convert_element_type.32), channel_id=1, source_target_pairs={{0,2},{1,3},{2,4},{3,5},{4,6},{5,7},{6,8},{7,9},{8,10},{9,11},{10,... | collective-permute-start | bytes 786440 | tf_op jit(solution)/shard_map/ppermute | solution.py:16
  137.0 6.9 %copy-start.4 = (bf16[4,384,128]{2,1,0:T(8,128)(2,1)}, bf16[4,384,128]{2,1,0:T(8,128)(2,1)S(1)}, u32[]{:S(2)}) copy-start(bf16[4,384,128]{2,1,0:T(8,128)(2,1)S(1)} %get-tuple-element.272) | copy-start | bytes 1179652 | tf_op jit(solution)/shard_map/while
  137.1 6.9 %copy-start.9 = (bf16[4,384,128]{2,1,0:T(8,128)(2,1)}, bf16[4,384,128]{2,1,0:T(8,128)(2,1)S(1)}, u32[]{:S(2)}) copy-start(bf16[4,384,128]{2,1,0:T(8,128)(2,1)S(1)} %get-tuple-element.271) | copy-start | bytes 1179652 | tf_op jit(solution)/shard_map/while
  160.7 4.0 copy-start.5
  160.7 4.0 copy-start.10
  164.7 6.9 %copy-start.4 = (bf16[4,384,128]{2,1,0:T(8,128)(2,1)}, bf16[4,384,128]{2,1,0:T(8,128)(2,1)S(1)}, u32[]{:S(2)}) copy-start(bf16[4,384,128]{2,1,0:T(8,128)(2,1)S(1)} %get-tuple-element.272) | copy-start | bytes 1179652 | tf_op jit(solution)/shard_map/while
  164.7 6.9 %copy-start.9 = (bf16[4,384,128]{2,1,0:T(8,128)(2,1)}, bf16[4,384,128]{2,1,0:T(8,128)(2,1)S(1)}, u32[]{:S(2)}) copy-start(bf16[4,384,128]{2,1,0:T(8,128)(2,1)S(1)} %get-tuple-element.271) | copy-start | bytes 1179652 | tf_op jit(solution)/shard_map/while
  188.4 4.0 copy-start.5
  188.4 4.0 copy-start.10
  192.4 6.9 %copy-start.4 = (bf16[4,384,128]{2,1,0:T(8,128)(2,1)}, bf16[4,384,128]{2,1,0:T(8,128)(2,1)S(1)}, u32[]{:S(2)}) copy-start(bf16[4,384,128]{2,1,0:T(8,128)(2,1)S(1)} %get-tuple-element.272) | copy-start | bytes 1179652 | tf_op jit(solution)/shard_map/while
  192.4 6.9 %copy-start.9 = (bf16[4,384,128]{2,1,0:T(8,128)(2,1)}, bf16[4,384,128]{2,1,0:T(8,128)(2,1)S(1)}, u32[]{:S(2)}) copy-start(bf16[4,384,128]{2,1,0:T(8,128)(2,1)S(1)} %get-tuple-element.271) | copy-start | bytes 1179652 | tf_op jit(solution)/shard_map/while
  216.1 4.0 copy-start.5
  216.1 4.0 copy-start.10
  220.1 6.9 %copy-start.4 = (bf16[4,384,128]{2,1,0:T(8,128)(2,1)}, bf16[4,384,128]{2,1,0:T(8,128)(2,1)S(1)}, u32[]{:S(2)}) copy-start(bf16[4,384,128]{2,1,0:T(8,128)(2,1)S(1)} %get-tuple-element.272) | copy-start | bytes 1179652 | tf_op jit(solution)/shard_map/while
  220.1 6.9 %copy-start.9 = (bf16[4,384,128]{2,1,0:T(8,128)(2,1)}, bf16[4,384,128]{2,1,0:T(8,128)(2,1)S(1)}, u32[]{:S(2)}) copy-start(bf16[4,384,128]{2,1,0:T(8,128)(2,1)S(1)} %get-tuple-element.271) | copy-start | bytes 1179652 | tf_op jit(solution)/shard_map/while
  243.8 4.0 copy-start.5
  243.8 4.0 copy-start.10
  249.7 35.1 %collective-permute-start.3 = (f32[128,1024]{0,1:T(8,128)}, f32[128,1024]{0,1:T(8,128)}, u32[]{:S(2)}, u32[]{:S(2)}) collective-permute-start(f32[128,1024]{0,1:T(8,128)} %get-tuple-element.157), channel_id=1, source_target_pairs={{2,0},{3,1},{4,2},{5,3},{6,4},{7,5},{8,6},{9,7},{10,8},{11,9},{12,... | collective-permute-start | bytes 1572872 | tf_op jit(solution)/shard_map/ppermute | solution.py:16
  251.0 33.8 %collective-permute-start.2 = (f32[128,1024]{0,1:T(8,128)S(1)}, f32[128,1024]{0,1:T(8,128)}, u32[]{:S(2)}, u32[]{:S(2)}) collective-permute-start(f32[128,1024]{0,1:T(8,128)S(1)} %get-tuple-element.156), channel_id=1, source_target_pairs={{1,0},{2,1},{3,2},{4,3},{5,4},{6,5},{7,6},{8,7},{9,8},{10,9},{11,1... | collective-permute-start | bytes 1572872 | tf_op jit(solution)/shard_map/ppermute | solution.py:16
  252.3 77.4 %copy-start.3 = (bf16[4,128,2048]{2,1,0:T(8,128)(2,1)S(1)}, bf16[4,128,2048]{2,1,0:T(8,128)(2,1)}, u32[]{:S(2)}) copy-start(bf16[4,128,2048]{2,1,0:T(8,128)(2,1)} %copy.38) | copy-start | bytes 6291460
  287.2 72.4 %all-gather.3.cloned.1.call-start = ((), (), s32[]{:S(2)}) async-start(), calls=%async_computation.4 | async-start | bytes 1310720 | tf_op jit(solution)/shard_map/all_gather | solution.py:106
  288.0 199.5 %all-reduce.2.cloned.1.call-start = ((), (), s32[]{:S(2)}) async-start(), calls=%async_computation.6 | async-start | bytes 16777216 | tf_op jit(solution)/shard_map/psum | solution.py:119
  368.6 50.8 %all-to-all-start.1 = ((bf16[4,128,2048]{2,1,0:T(8,128)(2,1)}), bf16[4,128,2048]{2,1,0:T(8,128)(2,1)S(1)}, u32[]{:S(2)}, u32[]{:S(2)}) async-start(bf16[4,128,2048]{2,1,0:T(8,128)(2,1)} %bitcast.18), calls=%async_computation.2 | async-start | bytes 4194304 | tf_op jit(solution)/shard_map/all_to_all | solution.py:111
  (2 other events, 5.2 us)
Sparse Core Ops, SparseCore 0:
  78.6 42.7 reduce-scatter.1
  287.3 42.3 all-gather.4
  331.3 28.2 all-gather.2
  362.9 124.4 all-reduce.1
where the time goes:
time: 504 us; the launch traced here: 503 us
  waiting for transfers between devices  301 us (60%)
  matrix products  130 us (26%)
  local copies, waits for them, and re-layouts  31 us (6%)
  starting transfers between devices  20.2 us (4%)
  between operations  13.9 us (3%)
  other arithmetic  6.91 us (1%)
    psum x1, waiting for transfers between devices, body(): weight_grad = lax.psum(shard_grad, 'seq')  66.5 us
    all_to_all x1, waiting for transfers between devices, body(): lax.all_to_all(hidden, 'fsdp', split_axis=1, concat_axis=0, tiled=True)  48.1 us
    reduce_scatter x1, waiting for transfers between devices, body(): lax.psum_scatter(jnp.dot(rows, weights, preferred_element_type=jnp.float3...  42.8 us
    all_to_all x1, waiting for transfers between devices, body(): lax.all_to_all(spread, 'fsdp', split_axis=0, concat_axis=1, tiled=True)  42.7 us
    all_gather x1, waiting for transfers between devices, body(): lax.all_gather(all_grad, 'fsdp', axis=0, tiled=True)  41.5 us
    ppermute x4, waiting for transfers between devices, shifted(): return lax.ppermute(block, axis, route)  35.6 us
    dot_general x4, matrix products, attend_group(): jnp.einsum('rhk,kd->rhd', dscores, kgrp, preferred_element_type=jnp.float32)  31.9 us
    dot_general x4, matrix products, attend_group(): jnp.einsum('rhk,rhd->kd', dscores, qgrp, preferred_element_type=jnp.float32)  30 us
  transfers between devices with their start and end apart: 10, of which 8 were waited for; matrix products, arithmetic and copies ran while one was open for 5% of the time, Pallas kernels for 0%

commit v1 on v0

--- a/solution.py
+++ b/solution.py
@@ -116,7 +116,11 @@
         (((0,), (0,)), ((), ())),
         preferred_element_type=jnp.float32,
     )
-    weight_grad = lax.psum(shard_grad, "seq")
+    weight_grad = shard_grad
+    for hop in (1, 2, 4):
+        weight_grad = weight_grad + lax.ppermute(
+            weight_grad, "seq", [(dev, dev ^ hop) for dev in range(8)]
+        )
     return (attn_out, grad_queries, grad_hidden, weight_grad)
 
 

time: 504 us -> 767 us (1.52)
  waiting for transfers between devices: 301 us -> 527 us
  other arithmetic: 6.91 us -> 42 us
    ppermute x0 -> x3, waiting for transfers between devices: none -> 286 us  [body(): lax.ppermute(weight_grad, 'seq', [(dev, dev ^ hop) for dev in range(8)])]
    psum x1 -> x0, waiting for transfers between devices: 66.5 us -> none  [body(): weight_grad = lax.psum(shard_grad, 'seq')]
    add x0 -> x3, other arithmetic: none -> 35.1 us  [body(): weight_grad + lax.ppermute(weight_grad, 'seq', [(dev, dev ^ hop) for dev...]
    unnamed x21 -> x23, local copies, waits for them, and re-layouts: 22.2 us -> 25.4 us
  transfers between devices with their start and end apart: 10 -> 12, of which waited for: 8 -> 10; matrix products, arithmetic and copies ran while one was open for 5% -> 2% of each run, Pallas kernels for 0% -> 0%
where the time goes in v1:
time: 767 us; the launch traced here: 765 us
  waiting for transfers between devices  527 us (69%)
  matrix products  127 us (17%)
  other arithmetic  42 us (5%)
  local copies, waits for them, and re-layouts  34.2 us (4%)
  starting transfers between devices  21.6 us (3%)
  between operations  13.9 us (2%)
    ppermute x3, waiting for transfers between devices, body(): lax.ppermute(weight_grad, 'seq', [(dev, dev ^ hop) for dev in range(8)])  286 us
    all_to_all x1, waiting for transfers between devices, body(): lax.all_to_all(hidden, 'fsdp', split_axis=1, concat_axis=0, tiled=True)  48.1 us
    reduce_scatter x1, waiting for transfers between devices, body(): lax.psum_scatter(jnp.dot(rows, weights, preferred_element_type=jnp.float3...  42.8 us
    all_to_all x1, waiting for transfers between devices, body(): lax.all_to_all(spread, 'fsdp', split_axis=0, concat_axis=1, tiled=True)  42.8 us
    all_gather x1, waiting for transfers between devices, body(): lax.all_gather(all_grad, 'fsdp', axis=0, tiled=True)  42.2 us
    ppermute x4, waiting for transfers between devices, shifted(): return lax.ppermute(block, axis, route)  35.6 us
    add x3, other arithmetic, body(): weight_grad + lax.ppermute(weight_grad, 'seq', [(dev, dev ^ hop) for dev...  35.1 us
    dot_general x4, matrix products, attend_group(): jnp.einsum('rhk,kd->rhd', dscores, kgrp, preferred_element_type=jnp.float32)  31.8 us
  transfers between devices with their start and end apart: 12, of which 10 were waited for; matrix products, arithmetic and copies ran while one was open for 2% of the time, Pallas kernels for 0%

profile of v1, /device:TPU:0, one launch (start us, length us, event | category | flops | bytes accessed | tf_op | source)
XLA Modules:
  0.0 765.4 jit_solution(6997137978436386233)
XLA Ops:
  7.2 4.1 copy.37
  11.2 6.5 all-to-all-start
  17.8 48.1 %all-to-all-done = bf16[128,4,2048]{0,2,1:T(8,128)(2,1)S(1)} async-done(((bf16[128,4,2048]{0,2,1:T(8,128)(2,1)}), bf16[128,4,2048]{0,2,1:T(8,128)(2,1)S(1)}, u32[]{:S(2)}, u32[]{:S(2)}) %all-to-all-start) | async-done | bytes 2097184 | tf_op jit(solution)/shard_map/all_to_all | solution.py:74
  69.1 4.2 copy-done
  74.4 4.0 convolution_bitcast_fusion.2
  78.5 42.8 %reduce-scatter.2.cloned.1.call-done = f32[128,1024]{0,1:T(8,128)} async-done(((f32[512,1024]{0,1:T(8,128)}), f32[128,1024]{0,1:T(8,128)}) %reduce-scatter.2.cloned.1.call-update) | async-done | bytes 524304 | tf_op jit(solution)/shard_map/reduce_scatter | solution.py:76
  125.0 4.3 collective-permute-start
  137.0 110.7 %while.17 = (s32[]{:T(128)}, bf16[4,128,8,128]{3,1,2,0:T(8,128)(2,1)}, bf16[4,128,8,128]{3,1,2,0:T(8,128)(2,1)}, f32[4,384,128]{1,2,0:T(8,128)S(1)}, f32[4,384,1...) while((s32[]{:T(128)}, ...), condition=%wide.region_5.6_spmd.clone, body=%wide.region_1.5_spmd.clone.sunk | while | flops 816830336 | bytes 25336436 | solution.py:57
  145.2 7.9 %fusion.155 = bf16[4,128,8,128]{3,1,2,0:T(8,128)(2,1)} fusion(bf16[4,128,8,128]{3,1,2,0:T(8,128)(2,1)} %get-tuple-element.254, s32[]{:T(128)S(6)} %copy.76, f32[128,8,384]{2,0,1:T(8,128)S(1)} %fusion.154, bf16[4,384,128]{2,1,0:T(8,128)(2,1)} %copy-done.10, f32[128,8,384]{2,0,1:T(8,128)} %get-tuple-element.238, f32[128,8]{0,1:T(8,128)S(1)} %get-tuple-element.237), kind=kOutput, calls=%fused_computation.16.clone.1 | convolution fusion | flops 103548288 | bytes 6661120 | tf_op jit(solution)/shard_map/while/body/eval_jaxpr/rhk,kd->rhd/dot_general | solution.py:40
  153.2 7.5 fusion.156
  160.8 4.0 fusion.157
  172.9 7.9 %fusion.155 = bf16[4,128,8,128]{3,1,2,0:T(8,128)(2,1)} fusion(bf16[4,128,8,128]{3,1,2,0:T(8,128)(2,1)} %get-tuple-element.254, s32[]{:T(128)S(6)} %copy.76, f32[128,8,384]{2,0,1:T(8,128)S(1)} %fusion.154, bf16[4,384,128]{2,1,0:T(8,128)(2,1)} %copy-done.10, f32[128,8,384]{2,0,1:T(8,128)} %get-tuple-element.238, f32[128,8]{0,1:T(8,128)S(1)} %get-tuple-element.237), kind=kOutput, calls=%fused_computation.16.clone.1 | convolution fusion | flops 103548288 | bytes 6661120 | tf_op jit(solution)/shard_map/while/body/eval_jaxpr/rhk,kd->rhd/dot_general | solution.py:40
  180.9 7.5 fusion.156
  188.4 4.0 fusion.157
  200.6 7.9 %fusion.155 = bf16[4,128,8,128]{3,1,2,0:T(8,128)(2,1)} fusion(bf16[4,128,8,128]{3,1,2,0:T(8,128)(2,1)} %get-tuple-element.254, s32[]{:T(128)S(6)} %copy.76, f32[128,8,384]{2,0,1:T(8,128)S(1)} %fusion.154, bf16[4,384,128]{2,1,0:T(8,128)(2,1)} %copy-done.10, f32[128,8,384]{2,0,1:T(8,128)} %get-tuple-element.238, f32[128,8]{0,1:T(8,128)S(1)} %get-tuple-element.237), kind=kOutput, calls=%fused_computation.16.clone.1 | convolution fusion | flops 103548288 | bytes 6661120 | tf_op jit(solution)/shard_map/while/body/eval_jaxpr/rhk,kd->rhd/dot_general | solution.py:40
  208.5 7.6 fusion.156
  228.3 7.9 %fusion.155 = bf16[4,128,8,128]{3,1,2,0:T(8,128)(2,1)} fusion(bf16[4,128,8,128]{3,1,2,0:T(8,128)(2,1)} %get-tuple-element.254, s32[]{:T(128)S(6)} %copy.76, f32[128,8,384]{2,0,1:T(8,128)S(1)} %fusion.154, bf16[4,384,128]{2,1,0:T(8,128)(2,1)} %copy-done.10, f32[128,8,384]{2,0,1:T(8,128)} %get-tuple-element.238, f32[128,8]{0,1:T(8,128)S(1)} %get-tuple-element.237), kind=kOutput, calls=%fused_computation.16.clone.1 | convolution fusion | flops 103548288 | bytes 6661120 | tf_op jit(solution)/shard_map/while/body/eval_jaxpr/rhk,kd->rhd/dot_general | solution.py:40
  236.2 7.5 fusion.156
  243.7 4.0 fusion.157
  252.3 32.5 %collective-permute-done.3 = f32[128,1024]{0,1:T(8,128)} collective-permute-done((f32[128,1024]{0,1:T(8,128)}, f32[128,1024]{0,1:T(8,128)}, u32[]{:S(2)}, u32[]{:S(2)}) %collective-permute-start.3) | collective-permute-done | bytes 524320 | tf_op jit(solution)/shard_map/ppermute | solution.py:16
  287.4 42.2 %all-gather.5.cloned.1.call-done = bf16[512,1024]{0,1:T(8,128)(2,1)} async-done(((bf16[128,1024]{0,1:T(8,128)(2,1)}), bf16[512,1024]{0,1:T(8,128)(2,1)}) %all-gather.5.cloned.1.call-update) | async-done | bytes 1048592 | tf_op jit(solution)/shard_map/all_gather | solution.py:115
  336.4 13.3 %collective-permute-done.4 = f32[2048,1024]{0,1:T(8,128)} collective-permute-done((f32[2048,1024]{0,1:T(8,128)S(1)}, f32[2048,1024]{0,1:T(8,128)}, u32[]{:S(2)}, u32[]{:S(2)}) %collective-permute-start.4) | collective-permute-done | bytes 8388640 | tf_op jit(solution)/shard_map/ppermute | solution.py:121
  349.7 11.7 %add.70 = f32[2048,1024]{0,1:T(8,128)} add(f32[2048,1024]{0,1:T(8,128)} %copy-done.2, f32[2048,1024]{0,1:T(8,128)} %collective-permute-done.4) | non-fusion elementwise | flops 2097152 | bytes 25165824 | tf_op jit(solution)/shard_map/add | solution.py:121
  362.1 182.1 %collective-permute-done.5 = f32[2048,1024]{0,1:T(8,128)} collective-permute-done((f32[2048,1024]{0,1:T(8,128)}, f32[2048,1024]{0,1:T(8,128)}, u32[]{:S(2)}, u32[]{:S(2)}) %collective-permute-start.5) | collective-permute-done | bytes 8388640 | tf_op jit(solution)/shard_map/ppermute | solution.py:121
  544.3 11.7 %add.71 = f32[2048,1024]{0,1:T(8,128)} add(f32[2048,1024]{0,1:T(8,128)} %add.70, f32[2048,1024]{0,1:T(8,128)} %collective-permute-done.5) | non-fusion elementwise | flops 2097152 | bytes 25165824 | tf_op jit(solution)/shard_map/add | solution.py:121
  556.7 29.0 %all-gather.3.cloned.1.call-done = bf16[512,1024]{0,1:T(8,128)(2,1)} async-done(((bf16[128,1024]{0,1:T(8,128)(2,1)}), bf16[512,1024]{0,1:T(8,128)(2,1)}) %all-gather.3.cloned.1.call-update) | async-done | bytes 1048592 | tf_op jit(solution)/shard_map/all_gather | solution.py:106
  585.7 9.0 %convolution_convert_fusion.1 = bf16[512,2048]{1,0:T(8,128)(2,1)} fusion(bf16[512,1024]{0,1:T(8,128)(2,1)} %all-gather.3.cloned.1.call-done, f32[256,8,8,128]{3,2,1,0:T(8,128)} %bitcast.157, bf16[2048,1024]{1,0:T(8,128)(2,1)} %param.8), kind=kOutput, calls=%fused_computation.65 | convolution fusion | flops 2154823680 | bytes 15728640 | tf_op jit(solution)/shard_map/dot_general | solution.py:105
  594.7 4.0 all-to-all-start.1
  602.9 42.8 %all-to-all-done.1 = bf16[4,128,2048]{2,1,0:T(8,128)(2,1)S(1)} async-done(((bf16[4,128,2048]{2,1,0:T(8,128)(2,1)}), bf16[4,128,2048]{2,1,0:T(8,128)(2,1)S(1)}, u32[]{:S(2)}, u32[]{:S(2)}) %all-to-all-start.1) | async-done | bytes 2097184 | tf_op jit(solution)/shard_map/all_to_all | solution.py:111
  647.2 90.8 %collective-permute-done.6 = f32[2048,1024]{0,1:T(8,128)} collective-permute-done((f32[2048,1024]{0,1:T(8,128)}, f32[2048,1024]{0,1:T(8,128)}, u32[]{:S(2)}, u32[]{:S(2)}) %collective-permute-start.6) | collective-permute-done | bytes 8388640 | tf_op jit(solution)/shard_map/ppermute | solution.py:121
  737.9 11.7 %add.72 = f32[2048,1024]{0,1:T(8,128)} add(f32[2048,1024]{0,1:T(8,128)} %add.71, f32[2048,1024]{0,1:T(8,128)} %collective-permute-done.6) | non-fusion elementwise | flops 2097152 | bytes 25165824 | tf_op jit(solution)/shard_map/add | solution.py:121
  749.6 9.2 %copy.49 = f32[2048,1024]{1,0:T(8,128)} copy(f32[2048,1024]{0,1:T(8,128)} %add.72) | data formatting | bytes 16777216
  (105 shorter events, 73.2 us)
Async XLA Ops:
  11.2 6.5 copy-start.12
  11.2 54.7 %all-to-all-start = ((bf16[128,4,2048]{0,2,1:T(8,128)(2,1)}), bf16[128,4,2048]{0,2,1:T(8,128)(2,1)S(1)}, u32[]{:S(2)}, u32[]{:S(2)}) async-start(bf16[128,4,2048]{0,2,1:T(8,128)(2,1)} %bitcast.160), calls=%async_computation | async-start | bytes 4194304 | tf_op jit(solution)/shard_map/all_to_all | solution.py:74
  17.7 103.6 %reduce-scatter.2.cloned.1.call-start = ((), (), s32[]{:S(2)}) async-start(), calls=%async_computation.3 | async-start | bytes 2621440 | tf_op jit(solution)/shard_map/reduce_scatter | solution.py:76
  68.5 4.9 copy-start.1
  68.5 5.9 copy-start.3
  69.1 4.3 copy-start
  78.4 50.9 %copy-start.7 = (bf16[128,4096]{1,0:T(8,128)(2,1)S(1)}, bf16[128,4096]{1,0:T(8,128)(2,1)}, u32[]{:S(2)}) copy-start(bf16[128,4096]{1,0:T(8,128)(2,1)} %param.10) | copy-start | bytes 3145732
  78.4 251.2 %all-gather.5.cloned.1.call-start = ((), (), s32[]{:S(2)}) async-start(), calls=%async_computation.5 | async-start | bytes 1310720 | tf_op jit(solution)/shard_map/all_gather | solution.py:115
  122.4 9.9 %collective-permute-start.1 = (bf16[128,1024]{0,1:T(8,128)(2,1)S(1)}, bf16[128,1024]{0,1:T(8,128)(2,1)S(1)}, u32[]{:S(2)}, u32[]{:S(2)}) collective-permute-start(bf16[128,1024]{0,1:T(8,128)(2,1)S(1)} %convert_element_type.32), channel_id=1, source_target_pairs={{0,1},{1,2},{2,3},{3,4},{4,5},{5,6},{6,7},{7,8},{8,9},{9,10},{10,1... | collective-permute-start | bytes 786440 | tf_op jit(solution)/shard_map/ppermute | solution.py:16
  125.0 10.4 %collective-permute-start = (bf16[128,1024]{0,1:T(8,128)(2,1)S(1)}, bf16[128,1024]{0,1:T(8,128)(2,1)}, u32[]{:S(2)}, u32[]{:S(2)}) collective-permute-start(bf16[128,1024]{0,1:T(8,128)(2,1)S(1)} %convert_element_type.32), channel_id=1, source_target_pairs={{0,2},{1,3},{2,4},{3,5},{4,6},{5,7},{6,8},{7,9},{8,10},{9,11},{10,... | collective-permute-start | bytes 786440 | tf_op jit(solution)/shard_map/ppermute | solution.py:16
  137.0 6.9 copy-start.5
  137.1 6.9 copy-start.10
  160.7 4.0 copy-start.6
  160.7 4.0 copy-start.11
  164.7 6.9 copy-start.5
  164.8 6.9 copy-start.10
  188.4 4.0 copy-start.6
  192.4 6.9 copy-start.5
  192.4 6.9 copy-start.10
  216.1 4.0 copy-start.6
  220.1 6.9 copy-start.5
  220.1 6.9 copy-start.10
  243.7 4.0 copy-start.6
  249.7 35.1 %collective-permute-start.3 = (f32[128,1024]{0,1:T(8,128)}, f32[128,1024]{0,1:T(8,128)}, u32[]{:S(2)}, u32[]{:S(2)}) collective-permute-start(f32[128,1024]{0,1:T(8,128)} %get-tuple-element.157), channel_id=1, source_target_pairs={{2,0},{3,1},{4,2},{5,3},{6,4},{7,5},{8,6},{9,7},{10,8},{11,9},{12,... | collective-permute-start | bytes 1572872 | tf_op jit(solution)/shard_map/ppermute | solution.py:16
  251.0 33.8 %collective-permute-start.2 = (f32[128,1024]{0,1:T(8,128)S(1)}, f32[128,1024]{0,1:T(8,128)}, u32[]{:S(2)}, u32[]{:S(2)}) collective-permute-start(f32[128,1024]{0,1:T(8,128)S(1)} %get-tuple-element.156), channel_id=1, source_target_pairs={{1,0},{2,1},{3,2},{4,3},{5,4},{6,5},{7,6},{8,7},{9,8},{10,9},{11,1... | collective-permute-start | bytes 1572872 | tf_op jit(solution)/shard_map/ppermute | solution.py:16
  252.3 77.4 %copy-start.4 = (bf16[4,128,2048]{2,1,0:T(8,128)(2,1)S(1)}, bf16[4,128,2048]{2,1,0:T(8,128)(2,1)}, u32[]{:S(2)}) copy-start(bf16[4,128,2048]{2,1,0:T(8,128)(2,1)} %copy.38) | copy-start | bytes 6291460
  287.1 298.6 %all-gather.3.cloned.1.call-start = ((), (), s32[]{:S(2)}) async-start(), calls=%async_computation.4 | async-start | bytes 1310720 | tf_op jit(solution)/shard_map/all_gather | solution.py:106
  336.4 13.3 %collective-permute-start.4 = (f32[2048,1024]{0,1:T(8,128)S(1)}, f32[2048,1024]{0,1:T(8,128)}, u32[]{:S(2)}, u32[]{:S(2)}) collective-permute-start(f32[2048,1024]{0,1:T(8,128)S(1)} %convolution_bitcast_fusion.1), channel_id=1, source_target_pairs={{0,4},{4,0},{8,12},{12,8},{16,20},{20,16},{24,28},{28,24},{1,5},{5... | collective-permute-start | bytes 25165832 | tf_op jit(solution)/shard_map/ppermute | solution.py:121
  361.4 182.8 %collective-permute-start.5 = (f32[2048,1024]{0,1:T(8,128)}, f32[2048,1024]{0,1:T(8,128)}, u32[]{:S(2)}, u32[]{:S(2)}) collective-permute-start(f32[2048,1024]{0,1:T(8,128)} %add.70), channel_id=1, source_target_pairs={{0,8},{4,12},{8,0},{12,4},{16,24},{20,28},{24,16},{28,20},{1,9},{5... | collective-permute-start | bytes 25165832 | tf_op jit(solution)/shard_map/ppermute | solution.py:121
  556.0 182.0 %collective-permute-start.6 = (f32[2048,1024]{0,1:T(8,128)}, f32[2048,1024]{0,1:T(8,128)}, u32[]{:S(2)}, u32[]{:S(2)}) collective-permute-start(f32[2048,1024]{0,1:T(8,128)} %add.71), channel_id=1, source_target_pairs={{0,16},{4,20},{8,24},{12,28},{16,0},{20,4},{24,8},{28,12},{1,17},{... | collective-permute-start | bytes 25165832 | tf_op jit(solution)/shard_map/ppermute | solution.py:121
  594.7 4.0 copy-start.9
  594.7 51.0 %all-to-all-start.1 = ((bf16[4,128,2048]{2,1,0:T(8,128)(2,1)}), bf16[4,128,2048]{2,1,0:T(8,128)(2,1)S(1)}, u32[]{:S(2)}, u32[]{:S(2)}) async-start(bf16[4,128,2048]{2,1,0:T(8,128)(2,1)} %bitcast.18), calls=%async_computation.2 | async-start | bytes 4194304 | tf_op jit(solution)/shard_map/all_to_all | solution.py:111
  (5 other events, 16.5 us)
Sparse Core Ops, SparseCore 0:
  78.6 42.7 reduce-scatter.1
  287.2 42.3 all-gather.4
  556.8 28.8 all-gather.2
